TPU v7x, 32 devices: a whole 2x2x4 slice. The times are simulated.
32 devices in a mesh: cache: 8 (over z, x), expert: 4 (over y, core).
Axes of the slice: x: 2, y: 2, z: 4, core: 2. Of those that a mesh axis runs over, the one named last changes fastest.
Arguments:
- query: bfloat16 [512, 2048], P('cache', 'expert'), may hold values from -8 to 8
- new_key: bfloat16 [512, 512], P('cache', 'expert'), may hold values from -8 to 8
- new_value: bfloat16 [512, 512], P('cache', 'expert'), may hold values from -6 to 6
- private_keys: bfloat16 [512, 64, 512], P('cache', None, 'expert'), may hold values from -8 to 8
- private_values: bfloat16 [512, 64, 512], P('cache', None, 'expert'), may hold values from -6 to 6
- private_lengths: int32 [512], P('cache'), may hold values from 1 to 64
- prefix_keys: bfloat16 [16, 1024, 512], P('cache', None, 'expert'), may hold values from -8 to 8
- prefix_values: bfloat16 [16, 1024, 512], P('cache', None, 'expert'), may hold values from -6 to 6
- slot_group: int32 [16], replicated, may hold values from 0 to 15, each once
- group_ids: int32 [512, 1], P('cache'), may hold values from 0 to 15; in each aligned block of 64 rows (0 to 63, 64 to 127, ...) at most 8 rows name the same one
- out_weight: bfloat16 [2048, 4096], P('expert', 'cache'), may hold values from -0.125 to 0.125
- hidden_in: bfloat16 [512, 4096], P(('cache', 'expert')), may hold values from -6 to 6
- norm_gain: float32 [4096], replicated, may hold values from 0.1 to 1.9
- expert_ids: int32 [512, 2], P(('cache', 'expert')), may hold values from 0 to 3, all different within a row; in each aligned block of 16 rows (0 to 15, 16 to 31, ...) at most 16 rows name the same one
- gate_weights: float32 [512, 2], P(('cache', 'expert')), may hold values from 0.1 to 0.9
- w_gate: bfloat16 [4, 4096, 14336], P('expert', None, 'cache'), may hold values from -0.09375 to 0.09375
- w_up: bfloat16 [4, 4096, 14336], P('expert', None, 'cache'), may hold values from -0.09375 to 0.09375
- w_down: bfloat16 [4, 14336, 4096], P('expert', 'cache'), may hold values from -0.046875 to 0.046875
Outputs:
- attention: bfloat16 [512, 2048], P('cache', 'expert')
- layer_out: bfloat16 [512, 4096], P(('cache', 'expert'))
Inputs may be any that keep to these rules, and one draw needn't show every extreme that they name: `group_ids`: within each aligned block of 64 requests at most 8 name one group. `slot_group`: each group is held by exactly one slot. `private_lengths`: positions 0 to length - 1 of a request's private cache are live. `expert_ids`: each token names two different experts; among the 16 tokens of one device at most 16 name one expert.
All inputs are finite; a program needn't handle non-finite values.
Results may differ from a plain program's by a relative error of at most 0.0095.
Values may be sent and summed in bfloat16 or wider, within the bound.
A program may use at most 128 MiB of HBM per device.

v0:
```python
import math

import jax
import jax.numpy as jnp
from jax import lax
from jax.sharding import PartitionSpec as P

MOSTG = 8


NEG = -1e30
EPSILON = 1e-05


def private_partial(queries, keys, values, lengths, new_key, new_value, scale):
    scores = jnp.einsum("rhd,rpd->rhp", queries, keys, preferred_element_type=jnp.float32) * scale
    live = jnp.arange(keys.shape[1], dtype=jnp.int32)[None, :] < lengths[:, None]
    scores = jnp.where(live[:, None, :], scores, NEG)
    fresh = jnp.einsum("rhd,rd->rh", queries, new_key, preferred_element_type=jnp.float32) * scale
    top = jnp.maximum(jnp.max(scores, axis=-1), fresh)
    expo = jnp.where(live[:, None, :], jnp.exp(scores - top[..., None]), 0.0)
    fresh_expo = jnp.exp(fresh - top)
    total = jnp.sum(expo, axis=-1) + fresh_expo
    summed = jnp.einsum(
        "rhp,rpd->rhd", expo.astype(jnp.bfloat16), values, preferred_element_type=jnp.float32
    )
    fresh_weight = lax.optimization_barrier(fresh_expo.astype(jnp.bfloat16)).astype(jnp.float32)
    summed = summed + fresh_weight[..., None] * new_value.astype(jnp.float32)[:, None, :]
    return (summed / total[..., None], top + jnp.log(total))


def prefix_partial(received, prefix_keys, prefix_values, scale):
    rows, heads, width = received.shape
    slots = prefix_keys.shape[0]
    blocks = received.reshape(rows // (slots * MOSTG), slots, MOSTG, heads, width)
    scores = (
        jnp.einsum("cgmhd,gpd->cgmhp", blocks, prefix_keys, preferred_element_type=jnp.float32)
        * scale
    )
    top = jnp.max(scores, axis=-1)
    expo = jnp.exp(scores - top[..., None])
    total = jnp.sum(expo, axis=-1)
    summed = jnp.einsum(
        "cgmhp,gpd->cgmhd",
        expo.astype(jnp.bfloat16),
        prefix_values,
        preferred_element_type=jnp.float32,
    )
    outputs = (summed / total[..., None]).reshape(rows, heads, width)
    return (outputs, (top + jnp.log(total)).reshape(rows, heads))


def on_device(
    query,
    new_key,
    new_value,
    private_keys,
    private_values,
    private_lengths,
    prefix_keys,
    prefix_values,
    slot_group,
    group_ids,
    out_weight,
    hidden_in,
    norm_gain,
    expert_ids,
    gate_weights,
    w_gate,
    w_up,
    w_down,
):
    head_dim = new_key.shape[1]
    requests = query.shape[0]
    heads = query.shape[1] // head_dim
    scale = 1.0 / math.sqrt(head_dim)
    queries = query.reshape(requests, heads, head_dim)
    near_out, near_lse = private_partial(
        queries, private_keys, private_values, private_lengths, new_key, new_value, scale
    )
    slot_count = slot_group.shape[0]
    matches = group_ids[:, 0][:, None] == slot_group[None, :]
    slot = jnp.sum(jnp.where(matches, jnp.arange(slot_count, dtype=jnp.int32)[None, :], 0), axis=1)
    order = jnp.arange(requests, dtype=jnp.int32)
    earlier = order[None, :] < order[:, None]
    rank = jnp.sum((slot[:, None] == slot[None, :]) & earlier, axis=1)
    position = slot * MOSTG + rank
    places = jnp.arange(slot_count * MOSTG, dtype=jnp.int32)
    placing = places[:, None] == position[None, :]
    sent = jnp.dot(placing.astype(jnp.bfloat16), query, preferred_element_type=jnp.float32).astype(
        jnp.bfloat16
    )
    sent = sent.reshape(slot_count * MOSTG, heads, head_dim)
    outputs, lse_part = prefix_partial(
        lax.all_to_all(sent, "cache", split_axis=0, concat_axis=0, tiled=True),
        prefix_keys,
        prefix_values,
        scale,
    )
    back_out = lax.all_to_all(outputs, "cache", split_axis=0, concat_axis=0, tiled=True)
    back_lse = lax.all_to_all(lse_part, "cache", split_axis=0, concat_axis=0, tiled=True)
    taking = placing.astype(jnp.float32)
    far_out = jnp.einsum("sr,shd->rhd", taking, back_out, precision=lax.Precision.HIGHEST)
    far_lse = jnp.einsum("sr,sh->rh", taking, back_lse, precision=lax.Precision.HIGHEST)
    both = jnp.logaddexp(near_lse, far_lse)
    merged = (
        near_out * jnp.exp(near_lse - both)[..., None]
        + far_out * jnp.exp(far_lse - both)[..., None]
    )
    attention = merged.astype(jnp.bfloat16).reshape(requests, heads * head_dim)
    experts = lax.axis_size("expert")
    tokens = hidden_in.shape[0]
    terms = jnp.dot(
        lax.all_gather(attention, "cache", axis=0, tiled=True),
        out_weight,
        preferred_element_type=jnp.float32,
    )
    regrouped = lax.all_to_all(
        terms.astype(jnp.bfloat16), "cache", split_axis=0, concat_axis=1, tiled=True
    ).astype(terms.dtype)
    proj = lax.psum_scatter(
        regrouped.astype(jnp.bfloat16), "expert", scatter_dimension=0, tiled=True
    ).astype(jnp.float32)
    resid = hidden_in.astype(jnp.float32) + proj
    normed = (
        resid * lax.rsqrt(jnp.mean(resid * resid, axis=-1, keepdims=True) + EPSILON) * norm_gain
    ).astype(jnp.bfloat16)
    capacity = max(2, 4 * tokens // experts)
    flat_ids = expert_ids.reshape(-1)
    order_ids = jnp.arange(flat_ids.shape[0], dtype=jnp.int32)
    before = order_ids[None, :] < order_ids[:, None]
    slot_rank = jnp.sum((flat_ids[:, None] == flat_ids[None, :]) & before, axis=1)
    destination = flat_ids * capacity + slot_rank
    expert_slots = jnp.arange(experts * capacity, dtype=jnp.int32)
    chosen = (destination[None, :] == expert_slots[:, None]).reshape(experts * capacity, tokens, 2)
    picking = jnp.sum(chosen.astype(jnp.bfloat16), axis=2)
    outgoing = jnp.dot(picking, normed, preferred_element_type=jnp.float32).astype(jnp.bfloat16)
    arrived = lax.all_to_all(outgoing, "expert", split_axis=0, concat_axis=0, tiled=True)
    piece = lax.all_gather(arrived, "cache", axis=0, tiled=True)
    gate = jnp.dot(piece, w_gate[0], preferred_element_type=jnp.float32)
    up = jnp.dot(piece, w_up[0], preferred_element_type=jnp.float32)
    act = (jax.nn.silu(gate) * up).astype(jnp.bfloat16)
    partial_out = jnp.dot(act, w_down[0], preferred_element_type=jnp.float32)
    summed_rows = lax.psum_scatter(
        partial_out.astype(jnp.bfloat16), "cache", scatter_dimension=0, tiled=True
    )
    returned = lax.all_to_all(summed_rows, "expert", split_axis=0, concat_axis=0, tiled=True)
    mixing = jnp.sum(jnp.where(chosen, gate_weights[None, :, :], 0.0), axis=2)
    moe = jnp.einsum(
        "st,sd->td", mixing, returned.astype(jnp.float32), precision=lax.Precision.HIGHEST
    )
    layer_out = (resid + moe).astype(jnp.bfloat16)
    return (attention, layer_out)


def solution(mesh):
    in_specs = (
        P("cache", "expert"),
        P("cache", "expert"),
        P("cache", "expert"),
        P("cache", None, "expert"),
        P("cache", None, "expert"),
        P("cache"),
        P("cache", None, "expert"),
        P("cache", None, "expert"),
        P(),
        P("cache", None),
        P("expert", "cache"),
        P(("cache", "expert"), None),
        P(),
        P(("cache", "expert"), None),
        P(("cache", "expert"), None),
        P("expert", None, "cache"),
        P("expert", None, "cache"),
        P("expert", "cache", None),
    )
    out_specs = (P("cache", "expert"), P(("cache", "expert"), None))
    return jax.shard_map(
        on_device, mesh=mesh, in_specs=in_specs, out_specs=out_specs, check_vma=False
    )
```

profile of v0, /device:TPU:0, one launch (start us, length us, event | category | flops | bytes accessed | tf_op | source)
XLA Modules:
  0.0 354.4 jit_solution(17689900936632118236)
XLA Ops:
  7.2 0.8 select_reduce_fusion.1
  8.0 0.2 convert_reduce_fusion
  8.2 1.1 convolution_convert_fusion.2
  9.4 0.7 reshape.100
  10.1 7.3 %all-to-all-start = ((bf16[128,4,128]{2,1,0:T(4,128)(2,1)}), bf16[128,4,128]{2,1,0:T(4,128)(2,1)S(1)}, u32[]{:S(2)}, u32[]{:S(2)}) async-start(bf16[128,4,128]{2,1,0:T(4,128)(2,1)} %reshape.100), calls=%async_computation | async-start | bytes 262144 | tf_op jit(solution)/shard_map/all_to_all | solution.py:95
  17.3 0.9 reshape.99
  18.2 0.7 iota_compare_fusion.4
  18.9 2.0 fusion.61
  20.9 0.9 fusion.45
  22.0 0.1 copy.110
  22.1 2.6 all-to-all-done
  24.7 1.6 bitcast_reduce_fusion
  26.3 0.5 fusion.17
  26.8 0.7 reshape.109
  27.5 3.4 all-to-all-start.1
  31.0 1.6 fusion.18
  32.6 0.9 copy.121
  33.5 4.1 %all-to-all-done.1 = f32[8,16,4]{1,2,0:T(4,128)S(1)} async-done(((f32[8,16,4]{1,2,0:T(4,128)}), f32[8,16,4]{1,2,0:T(4,128)S(1)}, u32[]{:S(2)}, u32[]{:S(2)}) %all-to-all-start.1) | async-done | bytes 2080 | tf_op jit(solution)/shard_map/all_to_all | solution.py:101
  37.5 3.4 all-to-all-start.2
  41.0 0.2 fusion.35
  41.3 0.1 copy.111
  41.5 0.2 subtract_exponential_fusion.1
  41.8 0.1 copy.113
  41.9 0.1 copy.123
  42.0 0.1 copy.119
  42.1 7.0 %all-to-all-done.2 = f32[128,4,128]{2,1,0:T(4,128)S(1)} async-done(((f32[128,4,128]{2,1,0:T(4,128)}), f32[128,4,128]{2,1,0:T(4,128)S(1)}, u32[]{:S(2)}, u32[]{:S(2)}) %all-to-all-start.2) | async-done | bytes 262176 | tf_op jit(solution)/shard_map/all_to_all | solution.py:100
  49.1 0.2 fusion.30
  49.4 0.5 fusion.23
  49.9 31.7 %all_gather.6 = bf16[512,512]{1,0:T(8,128)(2,1)S(1)} all-gather(bf16[64,512]{1,0:T(8,128)(2,1)S(1)} %bitcast.102), channel_id=1, replica_groups=mesh['cache'=8,'expert'=4] {'cache'}, dimensions={0}, use_global_device_ids=true | all-gather | bytes 589824 | tf_op jit(solution)/shard_map/all_gather | solution.py:114
  81.6 0.4 convolution_convert_fusion.1
  82.0 13.0 %all_to_all.62 = bf16[8,64,512]{2,1,0:T(8,128)(2,1)S(1)} all-to-all(bf16[8,64,512]{2,1,0:T(8,128)(2,1)S(1)} %bitcast.92), channel_id=1, replica_groups=mesh['cache'=8,'expert'=4] {'cache'}, dimensions={0} | all-to-all | bytes 1048576 | tf_op jit(solution)/shard_map/all_to_all | solution.py:118
  95.1 0.8 copy.136
  96.0 0.1 copy.126
  96.1 0.1 eq.80
  96.2 0.2 convert_reduce_fusion.1
  96.4 0.1 copy.127
  96.6 20.2 %reduce-scatter.3.cloned.1.call-done = bf16[16,4096]{1,0:T(8,128)(2,1)} async-done(((bf16[64,4096]{1,0:T(8,128)(2,1)}), bf16[16,4096]{1,0:T(8,128)(2,1)}) %reduce-scatter.3.cloned.1.call-update) | async-done | bytes 131088 | tf_op jit(solution)/shard_map/reduce_scatter | solution.py:121
  116.8 1.1 multiply_reduce_fusion
  117.9 1.2 convolution_convert_fusion
  119.1 11.9 %all_to_all.63 = bf16[4,16,4096]{2,1,0:T(8,128)(2,1)} all-to-all(bf16[4,16,4096]{2,1,0:T(8,128)(2,1)S(1)} %bitcast.96), channel_id=1, replica_groups=mesh['cache'=8,'expert'=4] {'expert'}, dimensions={0} | all-to-all | bytes 1048576 | tf_op jit(solution)/shard_map/all_to_all | solution.py:138
  131.0 0.2 reduce-scatter.5.cloned.1.call-start
  131.3 72.7 %all-gather.2.cloned.1.call-done = bf16[512,4096]{1,0:T(8,128)(2,1)} async-done(((bf16[64,4096]{1,0:T(8,128)(2,1)}), bf16[512,4096]{1,0:T(8,128)(2,1)}) %all-gather.2.cloned.1.call-update) | async-done | bytes 4194320 | tf_op jit(solution)/shard_map/all_gather | solution.py:139
  204.0 14.6 %fusion.4 = f32[512,1792]{1,0:T(8,128)} fusion(bf16[512,4096]{1,0:T(8,128)(2,1)} %all-gather.2.cloned.1.call-done, bf16[1,4096,1792]{2,1,0:T(8,128)(2,1)} %param.33), kind=kOutput, calls=%fused_computation.4 | convolution fusion | flops 7516192768 | bytes 22544384 | tf_op jit(solution)/shard_map/dot_general | solution.py:140
  218.6 28.7 %fusion.6 = bf16[512,4096]{1,0:T(8,128)(2,1)} fusion(bf16[1,1792,4096]{2,1,0:T(8,128)(2,1)} %param.35, f32[512,1792]{1,0:T(8,128)} %fusion.4, bf16[512,4096]{1,0:T(8,128)(2,1)} %all-gather.2.cloned.1.call-done, bf16[1,4096,1792]{2,1,0:T(8,128)(2,1)} %param.34), kind=kOutput, calls=%fused_computation.6 | convolution fusion | flops 15039987712 | bytes 41418752 | tf_op jit(solution)/shard_map/dot_general | solution.py:143
  247.3 87.4 %reduce-scatter.5.cloned.1.call-done = bf16[64,4096]{1,0:T(8,128)(2,1)} async-done(((bf16[512,4096]{1,0:T(8,128)(2,1)}), bf16[64,4096]{1,0:T(8,128)(2,1)}) %reduce-scatter.5.cloned.1.call-update) | async-done | bytes 524304 | tf_op jit(solution)/shard_map/reduce_scatter | solution.py:144
  334.6 3.5 all-to-all-start.5
  338.2 8.7 %all-to-all-done.5 = bf16[4,16,4096]{2,1,0:T(8,128)(2,1)S(1)} async-done(((bf16[4,16,4096]{2,1,0:T(8,128)(2,1)}), bf16[4,16,4096]{2,1,0:T(8,128)(2,1)S(1)}, u32[]{:S(2)}, u32[]{:S(2)}) %all-to-all-start.5) | async-done | bytes 524320 | tf_op jit(solution)/shard_map/all_to_all | solution.py:147
  346.9 1.0 fusion.9
  (43 shorter events, 0.9 us)
Async XLA Ops:
  7.2 42.2 %copy-start = (bf16[64,64,128]{2,1,0:T(8,128)(2,1)S(1)}, bf16[64,64,128]{2,1,0:T(8,128)(2,1)}, u32[]{:S(2)}) copy-start(bf16[64,64,128]{2,1,0:T(8,128)(2,1)} %param.22) | copy-start | bytes 3145732
  10.1 14.6 %all-to-all-start = ((bf16[128,4,128]{2,1,0:T(4,128)(2,1)}), bf16[128,4,128]{2,1,0:T(4,128)(2,1)S(1)}, u32[]{:S(2)}, u32[]{:S(2)}) async-start(bf16[128,4,128]{2,1,0:T(4,128)(2,1)} %reshape.100), calls=%async_computation | async-start | bytes 262144 | tf_op jit(solution)/shard_map/all_to_all | solution.py:95
  26.3 15.2 %copy-start.6 = (bf16[64,128]{1,0:T(8,128)(2,1)S(1)}, bf16[64,128]{1,0:T(8,128)(2,1)}, u32[]{:S(2)}) copy-start(bf16[64,128]{1,0:T(8,128)(2,1)} %param.20) | copy-start | bytes 49156
  27.5 10.0 %all-to-all-start.1 = ((f32[8,16,4]{1,2,0:T(4,128)}), f32[8,16,4]{1,2,0:T(4,128)S(1)}, u32[]{:S(2)}, u32[]{:S(2)}) async-start(f32[8,16,4]{1,2,0:T(4,128)} %reshape.109), calls=%async_computation.1 | async-start | bytes 32768 | tf_op jit(solution)/shard_map/all_to_all | solution.py:101
  32.6 49.0 %copy-start.4 = (bf16[512,512]{1,0:T(8,128)(2,1)S(1)}, bf16[512,512]{1,0:T(8,128)(2,1)}, u32[]{:S(2)}) copy-start(bf16[512,512]{1,0:T(8,128)(2,1)} %param.28) | copy-start | bytes 1572868
  37.5 11.6 %all-to-all-start.2 = ((f32[128,4,128]{2,1,0:T(4,128)}), f32[128,4,128]{2,1,0:T(4,128)S(1)}, u32[]{:S(2)}, u32[]{:S(2)}) async-start(f32[128,4,128]{2,1,0:T(4,128)} %copy.121), calls=%async_computation.2 | async-start | bytes 524288 | tf_op jit(solution)/shard_map/all_to_all | solution.py:100
  41.0 75.8 %reduce-scatter.3.cloned.1.call-start = ((), (), s32[]{:S(2)}) async-start(), calls=%async_computation.8 | async-start | bytes 655360 | tf_op jit(solution)/shard_map/reduce_scatter | solution.py:121
  49.4 46.6 %copy-start.8 = (s32[16,2]{0,1:T(2,128)S(1)}, s32[16,2]{0,1:T(2,128)}, u32[]{:S(2)}) copy-start(s32[16,2]{0,1:T(2,128)} %param.31) | copy-start | bytes 388
  49.4 67.4 %copy-start.2 = (bf16[16,4096]{1,0:T(8,128)(2,1)S(1)}, bf16[16,4096]{1,0:T(8,128)(2,1)}, u32[]{:S(2)}) copy-start(bf16[16,4096]{1,0:T(8,128)(2,1)} %param.29) | copy-start | bytes 393220
  49.4 68.4 %copy-start.7 = (f32[4096]{0:T(1024)S(1)}, f32[4096]{0:T(1024)}, u32[]{:S(2)}) copy-start(f32[4096]{0:T(1024)} %param.30) | copy-start | bytes 49156
  49.9 81.1 %copy-start.5 = (bf16[8,8,4,128]{3,1,2,0:T(8,128)(2,1)}, bf16[8,8,4,128]{3,1,2,0:T(8,128)(2,1)S(1)}, u32[]{:S(2)}) copy-start(bf16[8,8,4,128]{3,1,2,0:T(8,128)(2,1)S(1)} %copy.150) | copy-start | bytes 196612
  95.9 108.0 %all-gather.2.cloned.1.call-start = ((), (), s32[]{:S(2)}) async-start(), calls=%async_computation.9 | async-start | bytes 4718592 | tf_op jit(solution)/shard_map/all_gather | solution.py:139
  131.0 203.6 %reduce-scatter.5.cloned.1.call-start = ((), (), s32[]{:S(2)}) async-start(), calls=%async_computation.10 | async-start | bytes 4718592 | tf_op jit(solution)/shard_map/reduce_scatter | solution.py:144
  218.6 129.3 %copy-start.1 = (bf16[64,64,128]{2,1,0:T(8,128)(2,1)S(1)}, bf16[64,64,128]{2,1,0:T(8,128)(2,1)}, u32[]{:S(2)}) copy-start(bf16[64,64,128]{2,1,0:T(8,128)(2,1)} %param.22) | copy-start | bytes 3145732
  247.2 90.9 %copy-start.9 = (f32[16,2]{0,1:T(2,128)S(1)}, f32[16,2]{0,1:T(2,128)}, u32[]{:S(2)}) copy-start(f32[16,2]{0,1:T(2,128)} %param.32) | copy-start | bytes 388
  247.2 99.7 %copy-start.3 = (bf16[16,4096]{1,0:T(8,128)(2,1)S(1)}, bf16[16,4096]{1,0:T(8,128)(2,1)}, u32[]{:S(2)}) copy-start(bf16[16,4096]{1,0:T(8,128)(2,1)} %reduce-scatter.3.cloned.1.call-done) | copy-start | bytes 393220
  334.6 12.3 %all-to-all-start.5 = ((bf16[4,16,4096]{2,1,0:T(8,128)(2,1)}), bf16[4,16,4096]{2,1,0:T(8,128)(2,1)S(1)}, u32[]{:S(2)}, u32[]{:S(2)}) async-start(bf16[4,16,4096]{2,1,0:T(8,128)(2,1)} %bitcast.100), calls=%async_computation.7 | async-start | bytes 1048576 | tf_op jit(solution)/shard_map/all_to_all | solution.py:147
Sparse Core Ops, SparseCore 0:
  96.0 20.6 reduce-scatter.2
  131.2 72.7 all-gather.1
  247.4 87.2 reduce-scatter.4
where the time goes:
time: 355 us; the launch traced here: 354 us
  waiting for transfers between devices  203 us (57%)
  blocking collectives  56.6 us (16%)
  matrix products  54 us (15%)
  starting transfers between devices  17.9 us (5%)
  between operations  14 us (4%)
  local copies, waits for them, and re-layouts  5.2 us (1%)
  other arithmetic  3.97 us (1%)
    reduce_scatter x1, waiting for transfers between devices, on_device(): lax.psum_scatter(partial_out.astype(jnp.bfloat16), 'cache', scatter_dimen...  87.4 us
    all_gather x1, waiting for transfers between devices, on_device(): piece = lax.all_gather(arrived, 'cache', axis=0, tiled=True)  72.7 us
    all_gather x1, blocking collectives, on_device(): lax.all_gather(attention, 'cache', axis=0, tiled=True)  31.7 us
    dot_general x1, matrix products, on_device(): partial_out = jnp.dot(act, w_down[0], preferred_element_type=jnp.float32)  28.7 us
    reduce_scatter x1, waiting for transfers between devices, on_device(): lax.psum_scatter(regrouped.astype(jnp.bfloat16), 'expert', scatter_dimens...  20.2 us
    dot_general x1, matrix products, on_device(): gate = jnp.dot(piece, w_gate[0], preferred_element_type=jnp.float32)  14.6 us
    all_to_all x1, blocking collectives, on_device(): lax.all_to_all(terms.astype(jnp.bfloat16), 'cache', split_axis=0, concat_...  13 us
    all_to_all x1, blocking collectives, on_device(): lax.all_to_all(outgoing, 'expert', split_axis=0, concat_axis=0, tiled=True)  11.9 us
  transfers between devices with their start and end apart: 7, of which 7 were waited for; matrix products, arithmetic and copies ran while one was open for 2% of the time, Pallas kernels for 0%

commit v1 on v0

--- a/solution.py
+++ b/solution.py
@@ -48,6 +48,14 @@
     )
     outputs = (summed / total[..., None]).reshape(rows, heads, width)
     return (outputs, (top + jnp.log(total)).reshape(rows, heads))
+
+
+def split_in_three(values):
+    first = lax.reduce_precision(values, 8, 7)
+    rest = values - first
+    second = lax.reduce_precision(rest, 8, 7)
+    third = rest - second
+    return jnp.concatenate([first, second, third], axis=1).astype(jnp.bfloat16)
 
 
 def on_device(
@@ -97,11 +105,21 @@
         prefix_values,
         scale,
     )
-    back_out = lax.all_to_all(outputs, "cache", split_axis=0, concat_axis=0, tiled=True)
-    back_lse = lax.all_to_all(lse_part, "cache", split_axis=0, concat_axis=0, tiled=True)
-    taking = placing.astype(jnp.float32)
-    far_out = jnp.einsum("sr,shd->rhd", taking, back_out, precision=lax.Precision.HIGHEST)
-    far_lse = jnp.einsum("sr,sh->rh", taking, back_lse, precision=lax.Precision.HIGHEST)
+    places_count = slot_count * MOSTG
+    parts = split_in_three(lse_part)
+    lanes = jnp.pad(parts, ((0, 0), (0, head_dim - parts.shape[1])))
+    packet = jnp.concatenate(
+        [outputs.astype(jnp.bfloat16).reshape(places_count, heads * head_dim), lanes], axis=1
+    )
+    back = lax.all_to_all(packet, "cache", split_axis=0, concat_axis=0, tiled=True)
+    taken = jnp.dot(
+        placing.astype(jnp.bfloat16).T, back, preferred_element_type=jnp.float32
+    )
+    far_out = taken[:, : heads * head_dim].reshape(requests, heads, head_dim)
+    far_lse = jnp.sum(
+        taken[:, heads * head_dim : heads * head_dim + 3 * heads].reshape(requests, 3, heads),
+        axis=1,
+    )
     both = jnp.logaddexp(near_lse, far_lse)
     merged = (
         near_out * jnp.exp(near_lse - both)[..., None]
@@ -110,17 +128,26 @@
     attention = merged.astype(jnp.bfloat16).reshape(requests, heads * head_dim)
     experts = lax.axis_size("expert")
     tokens = hidden_in.shape[0]
+    caches = lax.axis_size("cache")
+    copies = jnp.broadcast_to(attention[None], (caches,) + attention.shape)
+    every = lax.all_to_all(copies, "cache", split_axis=0, concat_axis=0, tiled=True)
     terms = jnp.dot(
-        lax.all_gather(attention, "cache", axis=0, tiled=True),
+        every.reshape(caches * requests, heads * head_dim),
         out_weight,
         preferred_element_type=jnp.float32,
-    )
+    ).astype(jnp.bfloat16)
+    columns = terms.shape[1]
     regrouped = lax.all_to_all(
-        terms.astype(jnp.bfloat16), "cache", split_axis=0, concat_axis=1, tiled=True
-    ).astype(terms.dtype)
-    proj = lax.psum_scatter(
-        regrouped.astype(jnp.bfloat16), "expert", scatter_dimension=0, tiled=True
-    ).astype(jnp.float32)
+        terms.reshape(caches * experts, tokens, columns),
+        ("cache", "expert"),
+        split_axis=0,
+        concat_axis=0,
+        tiled=True,
+    )
+    summed_blocks = jnp.sum(
+        regrouped.reshape(caches, experts, tokens, columns).astype(jnp.float32), axis=1
+    )
+    proj = summed_blocks.transpose(1, 0, 2).reshape(tokens, caches * columns)
     resid = hidden_in.astype(jnp.float32) + proj
     normed = (
         resid * lax.rsqrt(jnp.mean(resid * resid, axis=-1, keepdims=True) + EPSILON) * norm_gain
@@ -136,14 +163,23 @@
     picking = jnp.sum(chosen.astype(jnp.bfloat16), axis=2)
     outgoing = jnp.dot(picking, normed, preferred_element_type=jnp.float32).astype(jnp.bfloat16)
     arrived = lax.all_to_all(outgoing, "expert", split_axis=0, concat_axis=0, tiled=True)
-    piece = lax.all_gather(arrived, "cache", axis=0, tiled=True)
-    gate = jnp.dot(piece, w_gate[0], preferred_element_type=jnp.float32)
-    up = jnp.dot(piece, w_up[0], preferred_element_type=jnp.float32)
-    act = (jax.nn.silu(gate) * up).astype(jnp.bfloat16)
-    partial_out = jnp.dot(act, w_down[0], preferred_element_type=jnp.float32)
-    summed_rows = lax.psum_scatter(
-        partial_out.astype(jnp.bfloat16), "cache", scatter_dimension=0, tiled=True
-    )
+    half = arrived.shape[0] // 2
+    pieces = [
+        lax.all_gather(part, "cache", axis=0, tiled=True)
+        for part in (arrived[:half], arrived[half:])
+    ]
+    done = []
+    for piece in pieces:
+        gate = jnp.dot(piece, w_gate[0], preferred_element_type=jnp.float32)
+        up = jnp.dot(piece, w_up[0], preferred_element_type=jnp.float32)
+        act = (jax.nn.silu(gate) * up).astype(jnp.bfloat16)
+        partial_out = jnp.dot(act, w_down[0], preferred_element_type=jnp.float32)
+        done.append(
+            lax.psum_scatter(
+                partial_out.astype(jnp.bfloat16), "cache", scatter_dimension=0, tiled=True
+            )
+        )
+    summed_rows = jnp.concatenate(done, axis=0)
     returned = lax.all_to_all(summed_rows, "expert", split_axis=0, concat_axis=0, tiled=True)
     mixing = jnp.sum(jnp.where(chosen, gate_weights[None, :, :], 0.0), axis=2)
     moe = jnp.einsum(

time: 355 us -> 350 us (0.986)
  blocking collectives: 56.6 us -> 25.9 us
  waiting for transfers between devices: 203 us -> 225 us
    all_gather x1 -> x0, blocking collectives: 31.7 us -> none  [on_device(): lax.all_gather(attention, 'cache', axis=0, tiled=True)]
    reduce_scatter x1 -> x2, waiting for transfers between devices: 87.4 us -> 118 us  [on_device(): lax.psum_scatter(partial_out.astype(jnp.bfloat16), 'cache', scatter_dimen...]
    reduce_scatter x1 -> x0, waiting for transfers between devices: 20.2 us -> none  [on_device(): lax.psum_scatter(regrouped.astype(jnp.bfloat16), 'expert', scatter_dimens...]
    dot_general x3 -> x4, matrix products: 0.91 us -> 20.4 us  [the longest x2 18.9 us: on_device(): up = jnp.dot(piece, w_up[0], preferred_element_type=jnp.float32)]
    dot_general x1 -> x2, matrix products: 28.7 us -> 10.6 us  [on_device(): partial_out = jnp.dot(act, w_down[0], preferred_element_type=jnp.float32)]
    all_to_all x2, waiting for transfers between devices: 11.1 us -> 21.9 us  [the longest x1 14.9 us: on_device(): lax.all_to_all(terms.reshape(caches * experts, tokens, columns), ('cache'...]
    dot_general x1 -> x2, matrix products: 14.6 us -> 17.1 us  [on_device(): gate = jnp.dot(piece, w_gate[0], preferred_element_type=jnp.float32)]
    all_gather x1 -> x2, waiting for transfers between devices: 72.7 us -> 71.9 us  [on_device(): lax.all_gather(part, 'cache', axis=0, tiled=True)]
  transfers between devices with their start and end apart: 7 -> 8, of which waited for: 7 -> 8; matrix products, arithmetic and copies ran while one was open for 2% -> 15% of each run, Pallas kernels for 0% -> 0%
where the time goes in v1:
time: 350 us; the launch traced here: 349 us
  waiting for transfers between devices  225 us (64%)
  matrix products  56.3 us (16%)
  blocking collectives  25.9 us (7%)
  starting transfers between devices  18.4 us (5%)
  between operations  14.2 us (4%)
  other arithmetic  5.8 us (2%)
  local copies, waits for them, and re-layouts  4.05 us (1%)
    reduce_scatter x2, waiting for transfers between devices, on_device(): lax.psum_scatter(partial_out.astype(jnp.bfloat16), 'cache', scatter_dimen...  118 us
    all_gather x2, waiting for transfers between devices, on_device(): lax.all_gather(part, 'cache', axis=0, tiled=True)  71.9 us
    dot_general x2, matrix products, on_device(): up = jnp.dot(piece, w_up[0], preferred_element_type=jnp.float32)  18.9 us
    dot_general x2, matrix products, on_device(): gate = jnp.dot(piece, w_gate[0], preferred_element_type=jnp.float32)  17.1 us
    all_to_all x1, waiting for transfers between devices, on_device(): lax.all_to_all(terms.reshape(caches * experts, tokens, columns), ('cache'...  14.9 us
    all_to_all x1, blocking collectives, on_device(): lax.all_to_all(copies, 'cache', split_axis=0, concat_axis=0, tiled=True)  14.7 us
    all_to_all x1, blocking collectives, on_device(): lax.all_to_all(outgoing, 'expert', split_axis=0, concat_axis=0, tiled=True)  11.2 us
    dot_general x2, matrix products, on_device(): partial_out = jnp.dot(act, w_down[0], preferred_element_type=jnp.float32)  10.6 us
  transfers between devices with their start and end apart: 8, of which 8 were waited for; matrix products, arithmetic and copies ran while one was open for 15% of the time, Pallas kernels for 0%

profile of v1, /device:TPU:0, one launch (start us, length us, event | category | flops | bytes accessed | tf_op | source)
XLA Modules:
  0.0 349.3 jit_solution(6895577044818567732)
XLA Ops:
  7.2 0.9 select_reduce_fusion.1
  8.0 0.2 convert_reduce_fusion.1
  8.2 1.0 convolution_convert_fusion.2
  9.2 0.7 reshape.120
  9.9 7.3 %all-to-all-start = ((bf16[128,4,128]{2,1,0:T(4,128)(2,1)}), bf16[128,4,128]{2,1,0:T(4,128)(2,1)S(1)}, u32[]{:S(2)}, u32[]{:S(2)}) async-start(bf16[128,4,128]{2,1,0:T(4,128)(2,1)} %reshape.120), calls=%async_computation | async-start | bytes 262144 | tf_op jit(solution)/shard_map/all_to_all | solution.py:103
  17.2 0.9 reshape.119
  18.1 0.7 iota_compare_fusion.4
  18.8 2.0 fusion.74
  20.8 0.2 fusion.60
  21.1 3.4 all-to-all-done
  24.6 1.6 bitcast_reduce_fusion
  26.1 0.5 fusion.32
  26.7 0.1 add.71
  26.9 0.1 copy.103
  27.0 1.6 fusion.35
  28.6 0.7 pad_maximum_fusion.1
  29.3 3.4 all-to-all-start.1
  32.8 0.2 fusion.50
  33.1 0.1 copy.83
  33.3 7.0 %all-to-all-done.1 = bf16[8,16,640]{2,1,0:T(8,128)(2,1)S(1)} async-done(((bf16[8,16,640]{2,1,0:T(8,128)(2,1)}), bf16[8,16,640]{2,1,0:T(8,128)(2,1)S(1)}, u32[]{:S(2)}, u32[]{:S(2)}) %all-to-all-start.1) | async-done | bytes 163872 | tf_op jit(solution)/shard_map/all_to_all | solution.py:114
  40.2 0.2 fusion.53
  41.0 0.5 fusion.40
  41.6 14.7 %all_to_all.45 = bf16[8,64,512]{2,1,0:T(8,128)(2,1)S(1)} all-to-all(bf16[8,64,512]{2,1,0:T(8,128)(2,1)S(1)} %broadcast_in_dim.45), channel_id=1, replica_groups=mesh['cache'=8,'expert'=4] {'cache'}, dimensions={0} | all-to-all | bytes 1048576 | tf_op jit(solution)/shard_map/all_to_all | solution.py:133
  56.3 1.2 convolution_convert_fusion.1
  57.5 3.7 %all-to-all-start.3 = ((bf16[32,16,512]{2,1,0:T(8,128)(2,1)}), bf16[32,16,512]{2,1,0:T(8,128)(2,1)S(1)}, u32[]{:S(2)}, u32[]{:S(2)}) async-start(bf16[32,16,512]{2,1,0:T(8,128)(2,1)} %bitcast.14), calls=%async_computation.3 | async-start | bytes 1048576 | tf_op jit(solution)/shard_map/all_to_all | solution.py:140
  61.5 0.2 convert_reduce_fusion.2
  61.9 14.9 %all-to-all-done.3 = bf16[32,16,512]{2,1,0:T(8,128)(2,1)S(1)} async-done(((bf16[32,16,512]{2,1,0:T(8,128)(2,1)}), bf16[32,16,512]{2,1,0:T(8,128)(2,1)S(1)}, u32[]{:S(2)}, u32[]{:S(2)}) %all-to-all-start.3) | async-done | bytes 524320 | tf_op jit(solution)/shard_map/all_to_all | solution.py:140
  77.0 0.2 multiply_reduce_fusion
  77.1 0.3 convolution_convert_fusion
  77.5 11.2 %all_to_all.46 = bf16[4,16,4096]{2,1,0:T(8,128)(2,1)S(1)} all-to-all(bf16[4,16,4096]{2,1,0:T(8,128)(2,1)S(1)} %bitcast.121), channel_id=1, replica_groups=mesh['cache'=8,'expert'=4] {'expert'}, dimensions={0} | all-to-all | bytes 1048576 | tf_op jit(solution)/shard_map/all_to_all | solution.py:165
  88.7 0.8 fusion.73
  89.6 0.7 all-gather.5.cloned.1.call-update
  90.3 0.2 reduce-scatter.3.cloned.1.call-start
  90.6 45.9 %all-gather.3.cloned.1.call-done = bf16[256,4096]{1,0:T(8,128)(2,1)} async-done(((bf16[32,4096]{1,0:T(8,128)(2,1)}), bf16[256,4096]{1,0:T(8,128)(2,1)}) %all-gather.3.cloned.1.call-update) | async-done | bytes 2097168 | tf_op jit(solution)/shard_map/all_gather | solution.py:168
  136.4 8.5 %fusion.10 = f32[256,1792]{1,0:T(8,128)S(1)} fusion(bf16[256,4096]{1,0:T(8,128)(2,1)} %all-gather.3.cloned.1.call-done, bf16[1,4096,1792]{2,1,0:T(8,128)(2,1)} %param.33), kind=kOutput, calls=%fused_computation.10 | convolution fusion | flops 3758096384 | bytes 18612224 | tf_op jit(solution)/shard_map/dot_general | solution.py:173
  145.0 9.5 %fusion.28 = bf16[256,1792]{1,0:T(8,128)(2,1)S(1)} fusion(bf16[256,4096]{1,0:T(8,128)(2,1)S(1)} %copy-done.10, bf16[1,4096,1792]{2,1,0:T(8,128)(2,1)} %param.34, f32[256,1792]{1,0:T(8,128)S(1)} %fusion.10), kind=kOutput, calls=%fused_computation.20 | convolution fusion | flops 3760848896 | bytes 19529728 | tf_op jit(solution)/shard_map/dot_general | solution.py:174
  154.5 5.3 %fusion.12 = bf16[256,4096]{1,0:T(8,128)(2,1)} fusion(bf16[256,1792]{1,0:T(8,128)(2,1)S(1)} %fusion.28, bf16[1,1792,4096]{2,1,0:T(8,128)(2,1)S(1)} %bitcast.136), kind=kOutput, calls=%fused_computation.12 | convolution fusion | flops 3759144960 | bytes 17694720 | tf_op jit(solution)/shard_map/dot_general | solution.py:176
  159.9 0.3 reduce-scatter.5.cloned.1.call-start
  160.2 26.0 %all-gather.5.cloned.1.call-done = bf16[256,4096]{1,0:T(8,128)(2,1)} async-done(((bf16[32,4096]{1,0:T(8,128)(2,1)}), bf16[256,4096]{1,0:T(8,128)(2,1)}) %all-gather.5.cloned.1.call-update) | async-done | bytes 2097168 | tf_op jit(solution)/shard_map/all_gather | solution.py:168
  186.2 8.5 %fusion.8 = f32[256,1792]{1,0:T(8,128)S(1)} fusion(bf16[256,4096]{1,0:T(8,128)(2,1)} %all-gather.5.cloned.1.call-done, bf16[1,4096,1792]{2,1,0:T(8,128)(2,1)} %param.33), kind=kOutput, calls=%fused_computation.8 | convolution fusion | flops 3758096384 | bytes 18612224 | tf_op jit(solution)/shard_map/dot_general | solution.py:173
  194.8 9.5 %fusion.25 = bf16[256,1792]{1,0:T(8,128)(2,1)S(1)} fusion(bf16[256,4096]{1,0:T(8,128)(2,1)S(1)} %copy-done.9, bf16[1,4096,1792]{2,1,0:T(8,128)(2,1)} %param.34, f32[256,1792]{1,0:T(8,128)S(1)} %fusion.8), kind=kOutput, calls=%fused_computation.19 | convolution fusion | flops 3760848896 | bytes 19529728 | tf_op jit(solution)/shard_map/dot_general | solution.py:174
  204.3 5.3 %fusion.15 = bf16[256,4096]{1,0:T(8,128)(2,1)} fusion(bf16[256,1792]{1,0:T(8,128)(2,1)S(1)} %fusion.25, bf16[1,1792,4096]{2,1,0:T(8,128)(2,1)S(1)} %bitcast.138), kind=kOutput, calls=%fused_computation.13 | convolution fusion | flops 3759144960 | bytes 17694720 | tf_op jit(solution)/shard_map/dot_general | solution.py:176
  209.6 47.1 %reduce-scatter.3.cloned.1.call-done = bf16[32,4096]{1,0:T(8,128)(2,1)} async-done(((bf16[256,4096]{1,0:T(8,128)(2,1)}), bf16[32,4096]{1,0:T(8,128)(2,1)}) %reduce-scatter.3.cloned.1.call-update) | async-done | bytes 262160 | tf_op jit(solution)/shard_map/reduce_scatter | solution.py:178
  256.7 70.9 %reduce-scatter.5.cloned.1.call-done = bf16[32,4096]{1,0:T(8,128)(2,1)} async-done(((bf16[256,4096]{1,0:T(8,128)(2,1)}), bf16[32,4096]{1,0:T(8,128)(2,1)}) %reduce-scatter.5.cloned.1.call-update) | async-done | bytes 262160 | tf_op jit(solution)/shard_map/reduce_scatter | solution.py:178
  327.6 1.9 pad_maximum_fusion
  329.5 3.5 all-to-all-start.5
  333.0 8.7 %all-to-all-done.5 = bf16[4,16,4096]{2,1,0:T(8,128)(2,1)S(1)} async-done(((bf16[4,16,4096]{2,1,0:T(8,128)(2,1)}), bf16[4,16,4096]{2,1,0:T(8,128)(2,1)S(1)}, u32[]{:S(2)}, u32[]{:S(2)}) %all-to-all-start.5) | async-done | bytes 524320 | tf_op jit(solution)/shard_map/all_to_all | solution.py:183
  341.7 1.0 fusion.18
  (83 shorter events, 1.8 us)
Async XLA Ops:
  7.2 33.8 %copy-start = (bf16[64,64,128]{2,1,0:T(8,128)(2,1)S(1)}, bf16[64,64,128]{2,1,0:T(8,128)(2,1)}, u32[]{:S(2)}) copy-start(bf16[64,64,128]{2,1,0:T(8,128)(2,1)} %param.22) | copy-start | bytes 3145732
  7.2 13.7 %copy-start.11 = (bf16[64,128]{1,0:T(8,128)(2,1)S(1)}, bf16[64,128]{1,0:T(8,128)(2,1)}, u32[]{:S(2)}) copy-start(bf16[64,128]{1,0:T(8,128)(2,1)} %param.19) | copy-start | bytes 49156
  9.9 14.6 %all-to-all-start = ((bf16[128,4,128]{2,1,0:T(4,128)(2,1)}), bf16[128,4,128]{2,1,0:T(4,128)(2,1)S(1)}, u32[]{:S(2)}, u32[]{:S(2)}) async-start(bf16[128,4,128]{2,1,0:T(4,128)(2,1)} %reshape.120), calls=%async_computation | async-start | bytes 262144 | tf_op jit(solution)/shard_map/all_to_all | solution.py:103
  27.0 6.2 %copy-start.6 = (bf16[64,128]{1,0:T(8,128)(2,1)S(1)}, bf16[64,128]{1,0:T(8,128)(2,1)}, u32[]{:S(2)}) copy-start(bf16[64,128]{1,0:T(8,128)(2,1)} %param.20) | copy-start | bytes 49156
  29.3 10.9 %all-to-all-start.1 = ((bf16[8,16,640]{2,1,0:T(8,128)(2,1)}), bf16[8,16,640]{2,1,0:T(8,128)(2,1)S(1)}, u32[]{:S(2)}, u32[]{:S(2)}) async-start(bf16[8,16,640]{2,1,0:T(8,128)(2,1)} %pad_maximum_fusion.1), calls=%async_computation.1 | async-start | bytes 327680 | tf_op jit(solution)/shard_map/all_to_all | solution.py:114
  41.0 15.3 %copy-start.3 = (bf16[512,512]{1,0:T(8,128)(2,1)S(1)}, bf16[512,512]{1,0:T(8,128)(2,1)}, u32[]{:S(2)}) copy-start(bf16[512,512]{1,0:T(8,128)(2,1)} %param.28) | copy-start | bytes 1572868
  41.5 16.0 %copy-start.4 = (bf16[8,8,4,128]{3,1,2,0:T(8,128)(2,1)}, bf16[8,8,4,128]{3,1,2,0:T(8,128)(2,1)S(1)}, u32[]{:S(2)}) copy-start(bf16[8,8,4,128]{3,1,2,0:T(8,128)(2,1)S(1)} %copy.115) | copy-start | bytes 196612
  41.5 19.8 %copy-start.7 = (s32[16,2]{0,1:T(2,128)S(1)}, s32[16,2]{0,1:T(2,128)}, u32[]{:S(2)}) copy-start(s32[16,2]{0,1:T(2,128)} %param.31) | copy-start | bytes 388
  56.3 20.7 %copy-start.2 = (bf16[16,4096]{1,0:T(8,128)(2,1)S(1)}, bf16[16,4096]{1,0:T(8,128)(2,1)}, u32[]{:S(2)}) copy-start(bf16[16,4096]{1,0:T(8,128)(2,1)} %param.29) | copy-start | bytes 393220
  56.3 20.9 %copy-start.5 = (f32[4096]{0:T(1024)S(1)}, f32[4096]{0:T(1024)}, u32[]{:S(2)}) copy-start(f32[4096]{0:T(1024)} %param.30) | copy-start | bytes 49156
  57.5 19.3 %all-to-all-start.3 = ((bf16[32,16,512]{2,1,0:T(8,128)(2,1)}), bf16[32,16,512]{2,1,0:T(8,128)(2,1)S(1)}, u32[]{:S(2)}, u32[]{:S(2)}) async-start(bf16[32,16,512]{2,1,0:T(8,128)(2,1)} %bitcast.14), calls=%async_computation.3 | async-start | bytes 1048576 | tf_op jit(solution)/shard_map/all_to_all | solution.py:140
  61.2 75.2 %all-gather.3.cloned.1.call-start = ((), (), s32[]{:S(2)}) async-start(), calls=%async_computation.8 | async-start | bytes 2359296 | tf_op jit(solution)/shard_map/all_gather | solution.py:168
  89.6 96.6 %all-gather.5.cloned.1.call-start = ((), (), s32[]{:S(2)}) async-start(), calls=%async_computation.10 | async-start | bytes 2359296 | tf_op jit(solution)/shard_map/all_gather | solution.py:168
  90.3 166.4 %reduce-scatter.3.cloned.1.call-start = ((), (), s32[]{:S(2)}) async-start(), calls=%async_computation.9 | async-start | bytes 2359296 | tf_op jit(solution)/shard_map/reduce_scatter | solution.py:178
  136.4 8.6 %copy-start.10 = (bf16[256,4096]{1,0:T(8,128)(2,1)S(1)}, bf16[256,4096]{1,0:T(8,128)(2,1)}, u32[]{:S(2)}) copy-start(bf16[256,4096]{1,0:T(8,128)(2,1)} %all-gather.3.cloned.1.call-done) | copy-start | bytes 6291460
  136.4 18.1 %slice-start = ((s8[14680064]{0:T(1024)(128)(4,1)}), s8[4194304]{0:T(1024)(128)(4,1)S(1)}, s32[]{:S(2)}) async-start(s8[14680064]{0:T(1024)(128)(4,1)} %bitcast.135), calls=%async_computation.12 | async-start | bytes 8388608
  136.4 18.1 %slice-start.1 = ((s8[14680064]{0:T(1024)(128)(4,1)}), s8[4194304]{0:T(1024)(128)(4,1)S(1)}, s32[]{:S(2)}) async-start(s8[14680064]{0:T(1024)(128)(4,1)} %bitcast.135), calls=%async_computation.13 | async-start | bytes 8388608
  145.0 9.5 %slice-start.2 = ((s8[14680064]{0:T(1024)(128)(4,1)}), s8[4194304]{0:T(1024)(128)(4,1)S(1)}, s32[]{:S(2)}) async-start(s8[14680064]{0:T(1024)(128)(4,1)} %bitcast.135), calls=%async_computation.14 | async-start | bytes 8388608
  145.0 9.5 %slice-start.3 = ((s8[14680064]{0:T(1024)(128)(4,1)}), s8[2097152]{0:T(1024)(128)(4,1)S(1)}, s32[]{:S(2)}) async-start(s8[14680064]{0:T(1024)(128)(4,1)} %bitcast.135), calls=%async_computation.15 | async-start | bytes 4194304
  159.9 167.7 %reduce-scatter.5.cloned.1.call-start = ((), (), s32[]{:S(2)}) async-start(), calls=%async_computation.11 | async-start | bytes 2359296 | tf_op jit(solution)/shard_map/reduce_scatter | solution.py:178
  186.2 8.6 %copy-start.9 = (bf16[256,4096]{1,0:T(8,128)(2,1)S(1)}, bf16[256,4096]{1,0:T(8,128)(2,1)}, u32[]{:S(2)}) copy-start(bf16[256,4096]{1,0:T(8,128)(2,1)} %all-gather.5.cloned.1.call-done) | copy-start | bytes 6291460
  186.2 18.1 %slice-start.4 = ((s8[14680064]{0:T(1024)(128)(4,1)}), s8[4194304]{0:T(1024)(128)(4,1)S(1)}, s32[]{:S(2)}) async-start(s8[14680064]{0:T(1024)(128)(4,1)} %bitcast.137), calls=%async_computation.16 | async-start | bytes 8388608
  186.2 18.1 %slice-start.5 = ((s8[14680064]{0:T(1024)(128)(4,1)}), s8[4194304]{0:T(1024)(128)(4,1)S(1)}, s32[]{:S(2)}) async-start(s8[14680064]{0:T(1024)(128)(4,1)} %bitcast.137), calls=%async_computation.17 | async-start | bytes 8388608
  194.8 9.5 %slice-start.6 = ((s8[14680064]{0:T(1024)(128)(4,1)}), s8[4194304]{0:T(1024)(128)(4,1)S(1)}, s32[]{:S(2)}) async-start(s8[14680064]{0:T(1024)(128)(4,1)} %bitcast.137), calls=%async_computation.18 | async-start | bytes 8388608
  194.8 9.5 %slice-start.7 = ((s8[14680064]{0:T(1024)(128)(4,1)}), s8[2097152]{0:T(1024)(128)(4,1)S(1)}, s32[]{:S(2)}) async-start(s8[14680064]{0:T(1024)(128)(4,1)} %bitcast.137), calls=%async_computation.19 | async-start | bytes 4194304
  209.6 123.4 %copy-start.8 = (f32[16,2]{0,1:T(2,128)S(1)}, f32[16,2]{0,1:T(2,128)}, u32[]{:S(2)}) copy-start(f32[16,2]{0,1:T(2,128)} %param.32) | copy-start | bytes 388
  209.6 133.1 %copy-start.1 = (bf16[64,64,128]{2,1,0:T(8,128)(2,1)S(1)}, bf16[64,64,128]{2,1,0:T(8,128)(2,1)}, u32[]{:S(2)}) copy-start(bf16[64,64,128]{2,1,0:T(8,128)(2,1)} %param.22) | copy-start | bytes 3145732
  329.5 12.3 %all-to-all-start.5 = ((bf16[4,16,4096]{2,1,0:T(8,128)(2,1)}), bf16[4,16,4096]{2,1,0:T(8,128)(2,1)S(1)}, u32[]{:S(2)}, u32[]{:S(2)}) async-start(bf16[4,16,4096]{2,1,0:T(8,128)(2,1)} %bitcast.23), calls=%async_computation.7 | async-start | bytes 1048576 | tf_op jit(solution)/shard_map/all_to_all | solution.py:183
Sparse Core Ops, SparseCore 0:
  89.7 46.6 all-gather.2
  138.5 47.6 all-gather.4
  189.7 66.9 reduce-scatter.2
  260.1 67.4 reduce-scatter.4
